TPU v7x, 32 devices: a whole 2x2x4 slice. The times are simulated.
32 devices in a mesh: gz: 32 (over z, y, x, core).
Axes of the slice: x: 2, y: 2, z: 4, core: 2. Of those that a mesh axis runs over, the one named last changes fastest.
Arguments:
- density: float32 [2, 32, 256, 256], P(None, 'gz'), may hold values from 0.02 to 0.8
- kernel_hat: float32 [64, 512, 512], P(None, 'gz'), may hold values from 0.37 to 7, as said below
Outputs:
- potential: float32 [2, 32, 256, 256], P(None, 'gz')
- energies: float32 [2], replicated
Inputs may be any that keep to these rules, and one draw needn't show every extreme that they name: kernel_hat at (a, b, c) equals kernel_hat at ((-a) mod 64, (-b) mod 512, (-c) mod 512).
All inputs are finite; a program needn't handle non-finite values.
Results may differ from a plain program's by a relative error of at most 0.00015.
Values sent between devices are 32-bit elements; how exact they have to be, the bound alone decides.
A program may use at most 64 MiB of HBM per device.

v0:
```python
import functools
import math

import jax
import jax.numpy as jnp
import numpy as np
from jax import lax
from jax.experimental import pallas as pl
from jax.experimental.pallas import tpu as pltpu
from jax.sharding import PartitionSpec as P

HGRID = 0.35
STENCIL = (0.8, -0.2, 4.0 / 105.0, -1.0 / 280.0)
KAPPA = 0.804
MU_X = 0.2195149727645171
BETA_C = 0.06672455060314922
GAMMA_C = 0.031090690869654894
FZ_CURV = 1.709921
PARAMS_UNPOL = (0.031091, 0.2137, 7.5957, 3.5876, 1.6382, 0.49294)
PARAMS_POL = (0.015545, 0.20548, 14.1189, 6.1977, 3.3662, 0.62517)
PARAMS_STIFF = (0.016887, 0.11125, 10.357, 3.6231, 0.88026, 0.49671)


def shifted(value, axis, steps):
    count = lax.axis_size(axis)
    leading, last = (max(0, -steps), min(count, count - steps))
    return lax.ppermute(value, axis, [(source, source + steps) for source in range(leading, last)])


def inner_slope(extended, direction):
    stencil_reach = len(STENCIL)
    length_out = extended.shape[direction] - 2 * stencil_reach
    result = 0.0
    for offset, weight in enumerate(STENCIL):
        upper_part = lax.slice_in_dim(
            extended,
            stencil_reach + offset + 1,
            stencil_reach + offset + 1 + length_out,
            axis=direction,
        )
        lower_part = lax.slice_in_dim(
            extended,
            stencil_reach - offset - 1,
            stencil_reach - offset - 1 + length_out,
            axis=direction,
        )
        result = result + weight * (upper_part - lower_part)
    return result / HGRID


def plane_slope(field, direction):
    stencil_reach = len(STENCIL)
    widths = [(0, 0)] * field.ndim
    widths[direction] = (stencil_reach, stencil_reach)
    return inner_slope(jnp.pad(field, widths), direction)


def pw_piece(radius, params):
    half_root = jnp.sqrt(radius)
    series = (
        params[2] * half_root
        + params[3] * radius
        + params[4] * radius * half_root
        + params[5] * radius * radius
    )
    return (
        -2.0 * params[0] * (1.0 + params[1] * radius) * jnp.log1p(1.0 / (2.0 * params[0] * series))
    )


def exchange_part(doubled, sigma_four):
    cube_root = jnp.cbrt(doubled)
    uniform_part = -0.75 * (3.0 / math.pi) ** (1.0 / 3.0) * cube_root
    reduced = sigma_four / (4.0 * (3.0 * math.pi**2) ** (2.0 / 3.0) * doubled**2 * cube_root**2)
    enhance = 1.0 + KAPPA - KAPPA / (1.0 + MU_X * reduced / KAPPA)
    return doubled * uniform_part * enhance


def energy_density(dens_up, dens_down, sigma_uu, sigma_ud, sigma_dd):
    exchange_term = 0.5 * exchange_part(2.0 * dens_up, 4.0 * sigma_uu) + 0.5 * exchange_part(
        2.0 * dens_down, 4.0 * sigma_dd
    )
    density_sum = dens_up + dens_down
    polarization = (dens_up - dens_down) / density_sum
    radius = jnp.cbrt(3.0 / (4.0 * math.pi * density_sum))
    plus_side = 1.0 + polarization
    minus_side = 1.0 - polarization
    plus_cube = jnp.cbrt(plus_side)
    minus_cube = jnp.cbrt(minus_side)
    spin_weight = (plus_side * plus_cube + minus_side * minus_cube - 2.0) / (
        2.0 ** (4.0 / 3.0) - 2.0
    )
    unpolar = pw_piece(radius, PARAMS_UNPOL)
    polarized = pw_piece(radius, PARAMS_POL)
    stiffness = pw_piece(radius, PARAMS_STIFF)
    polar_four = polarization**4
    local_corr = (
        unpolar
        - stiffness * spin_weight * (1.0 - polar_four) / FZ_CURV
        + (polarized - unpolar) * spin_weight * polar_four
    )
    phi_factor = 0.5 * (plus_cube**2 + minus_cube**2)
    phi_cubed = phi_factor**3
    screening_sq = 4.0 * jnp.cbrt(3.0 * math.pi**2 * density_sum) / math.pi
    sigma_total = sigma_uu + 2.0 * sigma_ud + sigma_dd
    scaled_sq = sigma_total / (4.0 * phi_factor**2 * screening_sq * density_sum**2)
    weight_a = BETA_C / GAMMA_C / jnp.expm1(-local_corr / (GAMMA_C * phi_cubed))
    gradient_term = (
        GAMMA_C
        * phi_cubed
        * jnp.log1p(
            BETA_C
            / GAMMA_C
            * scaled_sq
            * (1.0 + weight_a * scaled_sq)
            / (1.0 + weight_a * scaled_sq + weight_a**2 * scaled_sq**2)
        )
    )
    return exchange_term + density_sum * (local_corr + gradient_term)


def flux_pair(deriv_uu, deriv_ud, deriv_dd, gradient):
    return jnp.stack(
        [
            2.0 * deriv_uu * gradient[0] + deriv_ud * gradient[1],
            2.0 * deriv_dd * gradient[1] + deriv_ud * gradient[0],
        ]
    )


def xc_fields(dens, grad_z, grad_y, grad_x):
    sigma_uu = grad_z[0] * grad_z[0] + grad_y[0] * grad_y[0] + grad_x[0] * grad_x[0]
    sigma_ud = grad_z[0] * grad_z[1] + grad_y[0] * grad_y[1] + grad_x[0] * grad_x[1]
    sigma_dd = grad_z[1] * grad_z[1] + grad_y[1] * grad_y[1] + grad_x[1] * grad_x[1]
    energy, pullback = jax.vjp(energy_density, dens[0], dens[1], sigma_uu, sigma_ud, sigma_dd)
    d_up, d_down, d_uu, d_ud, d_dd = pullback(jnp.ones_like(energy))
    return (
        energy,
        jnp.stack([d_up, d_down]),
        flux_pair(d_uu, d_ud, d_dd, grad_z),
        flux_pair(d_uu, d_ud, d_dd, grad_y),
        flux_pair(d_uu, d_ud, d_dd, grad_x),
    )


MESH = pl.DeviceIdType.MESH
LANES = 128
SUBLANES = 8
VMEM_SPEC = pl.BlockSpec(memory_space=pltpu.VMEM)
VMEM_BYTES = 60 * 1024 * 1024


def extend_rows(field, depth):
    rows = field.shape[2]
    below_parts = []
    above_parts = []
    for distance in range(1, -(-depth // rows) + 1):
        needed = min(rows, depth - (distance - 1) * rows)
        below_parts.insert(0, shifted(field[:, :, rows - needed :], "gz", distance))
        above_parts.append(shifted(field[:, :, :needed], "gz", -distance))
    return jnp.concatenate(below_parts + [field] + above_parts, axis=2)


def split(value):
    high = value.astype(jnp.bfloat16)
    low = (value - high.astype(jnp.float32)).astype(jnp.bfloat16)
    return high, low


def np_split(table):
    table = np.asarray(table, np.float32)
    high = table.astype(jnp.bfloat16)
    low = (table - high.astype(np.float32)).astype(jnp.bfloat16)
    return high, low


def angles(spatial, spectral):
    index = np.outer(np.arange(spatial), np.arange(spectral)) % spectral
    return index * (2.0 * np.pi / spectral)


def y_tables(width_y, devices, scale):
    angle = angles(width_y, 2 * width_y)
    both = np.stack([np.cos(angle), -np.sin(angle)])
    both = both.reshape(2, width_y, devices, -1).transpose(2, 0, 3, 1)
    forward = both.reshape(4 * width_y, width_y)
    return np_split(forward), np_split(forward.T * scale)


def x_table(width_x):
    angle = angles(width_x, 2 * width_x)[:, :width_x]
    sine = np.sin(angle)
    sine[:, 0] = (-1.0) ** np.arange(width_x)
    return np_split(np.concatenate([np.cos(angle), sine], axis=1))


def z_tables(depth_z):
    angle = angles(depth_z, 2 * depth_z)
    cos, sin = np.cos(angle).T, np.sin(angle).T
    forward = np.block([[cos, sin], [-sin, cos]])
    out = []
    for table in (forward, forward.T):
        high, low = np_split(table)
        out.append(np.concatenate([high, high, low], axis=1))
    return out


def dot(left, right):
    return jnp.dot(left, right, preferred_element_type=jnp.float32)


def stacked(value):
    high, low = split(value)
    return jnp.concatenate([high, low, high], axis=0)


def greet(devices):
    me = lax.axis_index("gz")
    barrier = pltpu.get_barrier_semaphore()

    def signal(step, carry):
        pl.semaphore_signal(
            barrier,
            inc=1,
            device_id=(lax.rem(me + step, devices),),
            device_id_type=MESH,
        )
        return carry

    lax.fori_loop(1, devices, signal, 0)
    return lambda: pl.semaphore_wait(barrier, devices - 1)


def remote(devices, pieces, sends, receives):
    me = lax.axis_index("gz")

    def each(step, source_of, slot_of, act):
        for piece, (source, target) in enumerate(pieces):
            act(
                pltpu.make_async_remote_copy(
                    src_ref=source(source_of),
                    dst_ref=target(slot_of),
                    send_sem=sends.at[piece, step],
                    recv_sem=receives.at[piece, step],
                    device_id=(source_of,),
                    device_id_type=MESH,
                )
            )

    def start(step, carry):
        each(step, lax.rem(me + step, devices), me, lambda copy: copy.start())
        return carry

    def finish(step, carry):
        peer = lax.rem(me + step, devices)
        origin = lax.rem(me - step + devices, devices)
        each(step, peer, me, lambda copy: copy.wait_send())
        each(step, peer, origin, lambda copy: copy.wait_recv())
        return carry

    lax.fori_loop(1, devices, start, 0)
    return lambda: lax.fori_loop(1, devices, finish, 0)


def forward_kernel(devices, dens, t_high, t_low, dens_out, spec_out, spec, sends, receives):
    me = lax.axis_index("gz")
    arrived = greet(devices)
    width_y = t_high.shape[1]
    total = (dens[0] + dens[1]).reshape(width_y, dens.shape[3])
    high, low = split(total)
    values = dot(t_high[...], high) + (dot(t_high[...], low) + dot(t_low[...], high))
    spec[...] = values.reshape(spec.shape)
    arrived()
    finish = remote(
        devices,
        [
            (lambda peer: dens.at[:, peer], lambda slot: dens_out.at[:, slot]),
            (lambda peer: spec.at[peer], lambda slot: spec_out.at[slot]),
        ],
        sends,
        receives,
    )
    dens_out[:, me] = dens[:, me]
    spec_out[me] = spec[me]
    finish()


def forward_exchange(devices, dens, tables):
    width_x = dens.shape[3]
    spec_shape = (devices, tables[0].shape[0] // devices, width_x)
    return pl.pallas_call(
        functools.partial(forward_kernel, devices),
        out_shape=(
            jax.ShapeDtypeStruct(dens.shape, jnp.float32),
            jax.ShapeDtypeStruct(spec_shape, jnp.float32),
        ),
        in_specs=[VMEM_SPEC] * 3,
        out_specs=(VMEM_SPEC, VMEM_SPEC),
        scratch_shapes=[
            pltpu.VMEM(spec_shape, jnp.float32),
            pltpu.SemaphoreType.DMA((2, devices)),
            pltpu.SemaphoreType.DMA((2, devices)),
        ],
        compiler_params=pltpu.CompilerParams(
            collective_id=0, has_side_effects=True, vmem_limit_bytes=VMEM_BYTES
        ),
        name="forward_exchange",
    )(dens, *tables)


def filter_kernel(spec, kernel_hat, edge, tx_high, tx_low, z_fore, z_back, out, energy, held, wide):
    depth, rows, width = spec.shape
    count = rows // 2
    for q in range(count):
        held[q, :depth] = spec[:, q, :]
        held[q, depth:] = spec[:, count + q, :]

    def times_x(value):
        high, low = split(value.reshape(count * 2 * depth, width))
        result = dot(high, tx_high[...]) + (dot(low, tx_high[...]) + dot(high, tx_low[...]))
        wide[...] = result.reshape(wide.shape)

    lane = lax.broadcasted_iota(jnp.int32, (1, width), 1)
    first = lane == 0
    weight = jnp.where(first, 1.0, 2.0)
    alternate = jnp.where(lane % 2 == 0, 1.0, -1.0)
    edge_lane = lax.broadcasted_iota(jnp.int32, (1, LANES), 1)
    times_x(held[...])
    last = jnp.zeros((2 * depth, LANES), jnp.float32)
    back = []
    for q in range(count):
        cos_part = wide[q, :, :width]
        sin_part = wide[q, :, width:]
        last = jnp.where(edge_lane == q, sin_part[:, :1], last)
        sin_part = jnp.where(first, 0.0, sin_part)
        value = jnp.concatenate(
            [cos_part[:depth] + sin_part[depth:], cos_part[depth:] - sin_part[:depth]], axis=0
        )
        value = dot(z_fore[...], stacked(value))
        factor = kernel_hat[:, q, :] * weight
        value = value * jnp.concatenate([factor, factor], axis=0)
        wide[q, :, :width] = dot(z_back[...], stacked(value))
    last = dot(z_fore[...], stacked(last))
    last = last * jnp.concatenate([edge[...], edge[...]], axis=0)
    last = dot(z_back[...], stacked(last))
    times_x(wide[:, :, :width])
    acc = jnp.zeros((depth, width), jnp.float32)
    for q in range(count):
        cos_part = wide[q, :, :width] + last[:, q : q + 1] * alternate
        sin_part = jnp.where(first, 0.0, wide[q, :, width:])
        real = cos_part[:depth] - sin_part[depth:]
        imag = cos_part[depth:] + sin_part[:depth]
        acc = acc + (held[q, :depth] * real + held[q, depth:] * imag)
        out[:, q, :] = real
        out[:, count + q, :] = imag
    energy[...] = jnp.full(energy.shape, jnp.sum(acc))


def filtered(spec, kernel_hat):
    depth, rows, width = spec.shape
    count = rows // 2
    edge = jnp.pad(kernel_hat[:, :, width], ((0, 0), (0, LANES - count)))
    tables = (*x_table(width), *z_tables(depth))
    whole = [pl.BlockSpec(array.shape, lambda i, r=array.ndim: (0,) * r) for array in tables]
    return pl.pallas_call(
        filter_kernel,
        grid=(1,),
        out_shape=(
            jax.ShapeDtypeStruct(spec.shape, jnp.float32),
            jax.ShapeDtypeStruct((SUBLANES, LANES), jnp.float32),
        ),
        in_specs=[
            pl.BlockSpec(spec.shape, lambda i: (0, 0, 0)),
            pl.BlockSpec((2 * depth, count, width), lambda i: (0, 0, 0)),
            pl.BlockSpec(edge.shape, lambda i: (0, 0)),
            *whole,
        ],
        out_specs=(
            pl.BlockSpec(spec.shape, lambda i: (0, 0, 0)),
            pl.BlockSpec((SUBLANES, LANES), lambda i: (0, 0)),
        ),
        scratch_shapes=[
            pltpu.VMEM((count, 2 * depth, width), jnp.float32),
            pltpu.VMEM((count, 2 * depth, 2 * width), jnp.float32),
        ],
        compiler_params=pltpu.CompilerParams(vmem_limit_bytes=VMEM_BYTES),
        cost_estimate=pl.CostEstimate(
            flops=10**10, bytes_accessed=4 * 10**6, transcendentals=0
        ),
        name="kernel_filter",
    )(spec, kernel_hat, edge, *tables)


def backward_kernel(
    devices, spec, v_rows, partial, t_high, t_low, v_out, h_out, e_out, gathered, sums, sends, receives
):
    me = lax.axis_index("gz")
    arrived = greet(devices)
    arrived()
    finish = remote(
        devices,
        [
            (lambda peer: spec.at[peer], lambda slot: gathered.at[slot]),
            (lambda peer: v_rows.at[:, peer], lambda slot: v_out.at[:, slot]),
            (lambda peer: partial, lambda slot: sums.at[slot]),
        ],
        sends,
        receives,
    )
    gathered[me] = spec[me]
    v_out[:, me] = v_rows[:, me]
    sums[me] = partial[...]
    finish()
    high, low = split(gathered[...].reshape(t_high.shape[1], spec.shape[2]))
    h_out[...] = dot(t_high[...], high) + (dot(t_high[...], low) + dot(t_low[...], high))
    e_out[...] = jnp.sum(sums[...], axis=0)


def backward_exchange(devices, spec, v_rows, partial, tables):
    width_y = tables[0].shape[0]
    return pl.pallas_call(
        functools.partial(backward_kernel, devices),
        out_shape=(
            jax.ShapeDtypeStruct(v_rows.shape, jnp.float32),
            jax.ShapeDtypeStruct((width_y, spec.shape[2]), jnp.float32),
            jax.ShapeDtypeStruct(partial.shape, jnp.float32),
        ),
        in_specs=[VMEM_SPEC] * 5,
        out_specs=(VMEM_SPEC,) * 3,
        scratch_shapes=[
            pltpu.VMEM(spec.shape, jnp.float32),
            pltpu.VMEM((devices, *partial.shape), jnp.float32),
            pltpu.SemaphoreType.DMA((3, devices)),
            pltpu.SemaphoreType.DMA((3, devices)),
        ],
        compiler_params=pltpu.CompilerParams(
            collective_id=1, has_side_effects=True, vmem_limit_bytes=VMEM_BYTES
        ),
        name="backward_exchange",
    )(spec, v_rows, partial, *tables)


def xc_rows(dens):
    stencil_reach = len(STENCIL)
    grad_z = plane_slope(dens, 1)
    grad_x = plane_slope(dens, 3)
    grad_y = inner_slope(extend_rows(dens, stencil_reach), 2)
    energy, d_dens, flux_z, flux_y, flux_x = xc_fields(dens, grad_z, grad_y, grad_x)
    divergence_y = inner_slope(extend_rows(flux_y, stencil_reach), 2)
    v_xc = d_dens - (plane_slope(flux_z, 1) + divergence_y + plane_slope(flux_x, 3))
    return v_xc, jnp.sum(energy)


def per_device(density, kernel_hat):
    planes, width_y, width_x = density.shape[1:]
    devices = lax.axis_size("gz")
    assert planes == 1
    depth_z = planes * devices
    cell_count = depth_z * width_y * width_x
    forward, inverse = y_tables(width_y, devices, 1.0 / (8 * cell_count))
    dens, spec = forward_exchange(
        devices, density.reshape(2, devices, width_y // devices, width_x), forward
    )
    v_rows, energy_xc = xc_rows(dens)
    back, energy_h = filtered(spec, kernel_hat)
    row = lax.broadcasted_iota(jnp.int32, energy_h.shape, 0)
    partial = jnp.where(
        row == 0, energy_xc / cell_count, energy_h * (0.5 / (8.0 * cell_count) / cell_count)
    )
    v_xc, hartree, sums = backward_exchange(devices, back, v_rows, partial, inverse)
    potential = v_xc.reshape(2, 1, width_y, width_x) + hartree[None, None]
    return (potential, sums[:2, 0])


def solution(mesh):
    placed = (P(None, "gz", None, None), P(None, "gz", None))
    return jax.shard_map(
        per_device,
        mesh=mesh,
        in_specs=placed,
        out_specs=(P(None, "gz", None, None), P()),
        check_vma=False,
    )
```

profile of v0, /device:TPU:15, one launch (start us, length us, event | category | flops | bytes accessed | tf_op | source)
XLA Modules:
  0.0 143.5 jit_solution(3716537352798469693)
XLA Ops:
  0.6 0.0 slice-start
  0.6 45.6 %forward_exchange.1 = (f32[2,32,8,256]{3,2,1,0:T(8,128)}, f32[32,32,256]{2,1,0:T(8,128)}) custom-call(f32[2,32,8,256]{3,2,1,0:T(8,128)} %bitcast.102, bf16[1024,256]{1,0:T(8,128)(2,1)} %constant.168.clone.t_high, bf16[1024,256]{1,0:T(8,128)(2,1)} %constant.169.clone.t_low), custom_call_target="tpu_custom_call" | custom-call | tf_op jit(solution)/shard_map/forward_exchange/pallas_call | solution.py:291
  46.3 1.3 fusion.200
  47.6 1.9 %collective-permute-start = (f32[2,32,4,256]{3,2,1,0:T(4,128)S(1)}, f32[2,32,4,256]{3,2,1,0:T(4,128)S(1)}, u32[]{:S(2)}, u32[]{:S(2)}) collective-permute-start(f32[2,32,4,256]{3,2,1,0:T(4,128)S(1)} %get-tuple-element.46), channel_id=1, source_target_pairs={{1,0},{2,1},{3,2},{4,3},{5,4},{6,5},{7,6},{8,7},{9,8},{10,9},{11,1... | collective-permute-start | bytes 786440 | tf_op jit(solution)/shard_map/ppermute | solution.py:27
  49.5 5.4 %collective-permute-start.1 = (f32[2,32,4,256]{3,2,1,0:T(4,128)S(1)}, f32[2,32,4,256]{3,2,1,0:T(4,128)S(1)}, u32[]{:S(2)}, u32[]{:S(2)}) collective-permute-start(f32[2,32,4,256]{3,2,1,0:T(4,128)S(1)} %get-tuple-element.47), channel_id=1, source_target_pairs={{0,1},{1,2},{2,3},{3,4},{4,5},{5,6},{6,7},{7,8},{8,9},{9,10},{10,1... | collective-permute-start | bytes 786440 | tf_op jit(solution)/shard_map/ppermute | solution.py:27
  54.9 0.0 slice-done
  54.9 0.4 copy.16
  55.4 0.6 pad.18.edge
  56.0 0.0 copy-start
  56.0 7.1 %kernel_filter.1 = (f32[32,32,256]{2,1,0:T(8,128)}, f32[8,128]{1,0:T(8,128)}) custom-call(f32[32,32,256]{2,1,0:T(8,128)} %get-tuple-element.9.spec, f32[64,16,512]{2,1,0:T(8,128)} %kernel_hat.1, f32[64,128]{1,0:T(8,128)} %pad.18.edge, bf16[256,512]{1,0:T(8,128)(2,1)} %constant.170.clone.tx_high, bf16[256,512]{1,0:T(8,128)(2,1)} %constant.171.clone.tx_low, ...), custom_call_target="tpu_custom_call" | custom-call | flops 10000000000 | bytes 4000000 | tf_op jit(solution)/shard_map/kernel_filter/pallas_call | solution.py:365
  63.1 0.0 copy-done
  63.1 0.1 constant_dynamic-update-slice_fusion.1
  63.2 0.0 collective-permute-done
  63.2 0.1 constant_dynamic-update-slice_fusion
  63.2 0.0 collective-permute-done.1
  63.3 1.9 %fusion.31 = (f32[2,32,8,256]{3,2,1,0:T(8,128)S(1)}, f32[2,32,8,256]{3,2,1,0:T(8,128)S(1)}, f32[2,32,8,256]{3,2,1,0:T(8,128)S(1)}) fusion(f32[2,32,8,256]{3,2,1,0:T(8,128)S(1)} %copy-done, f32[2,32,4,256]{3,2,1,0:T(4,128)S(1)} %collective-permute-done.1, f32[2,32,12,256]{3,2,1,0:T(8,128)S(1)} %constant_dynamic-update-slice_fusion), kind=kLoop, calls=%fused_computation.61 | loop fusion | flops 5242880 | bytes 4456448 | tf_op jit(solution)/shard_map/div | solution.py:48
  65.2 3.6 %fusion.149 = (f32[]{:T(128)}, f32[1,32,8,256]{3,2,1,0:T(8,128)S(1)}, f32[1,32,8,256]{3,2,1,0:T(8,128)S(1)}, f32[1,32,8,256]{3,2,1,0:T(8,128)S(1)}, f32[1,32,8,256]{3,2,1,0:T(8,128)S(1)}) fusion(f32[2,32,8,256]{3,2,1,0:T(8,128)S(1)} %copy-done, f32[2,32,8,256]{3,2,1,0:T(8,128)S(1)} %get-tuple-element.44, f32[2,32,8,256]{3,2,1,0:T(8,128)S(1)} %get-tuple-element.43, ...), kind=kLoop, calls=%fused_computation.229 | loop fusion | flops 9633791 | bytes 3145732 | tf_op jit(solution)/shard_map/reduce_sum | solution.py:451
  68.8 1.6 %negate_divide_fusion = (f32[1,32,8,256]{3,2,1,0:T(8,128)S(1)}, f32[1,32,8,256]{3,2,1,0:T(8,128)S(1)}) fusion(f32[1,32,8,256]{3,2,1,0:T(8,128)S(1)} %get-tuple-element.20, f32[2,32,8,256]{3,2,1,0:T(8,128)S(1)} %copy-done), kind=kLoop, calls=%fused_computation.331 | loop fusion | flops 4980736 | bytes 1310720 | tf_op jit(solution)/shard_map/jvp()/div | solution.py:107
  70.3 5.0 %multiply_add_fusion.8 = (f32[1,32,8,256]{3,2,1,0:T(8,128)S(1)}, f32[1,32,8,256]{3,2,1,0:T(8,128)S(1)}, f32[1,32,8,256]{3,2,1,0:T(8,128)S(1)}, f32[1,32,8,256]{3,2,1,0:T(8,128)S(1)}) fusion(f32[1,32,8,256]{3,2,1,0:T(8,128)S(1)} %get-tuple-element.17, f32[2,32,8,256]{3,2,1,0:T(8,128)S(1)} %copy-done, f32[1,32,8,256]{3,2,1,0:T(8,128)S(1)} %get-tuple-element.20, ...), kind=kLoop, calls=%fused_computation.273 | loop fusion | flops 22478848 | bytes 2883584 | tf_op jit(solution)/shard_map/transpose(jvp())/add_any | solution.py:80
  75.3 1.8 %multiply_add_fusion.5 = (f32[1,32,8,256]{3,2,1,0:T(8,128)S(1)}, f32[1,32,8,256]{3,2,1,0:T(8,128)S(1)}, f32[1,32,8,256]{3,2,1,0:T(8,128)S(1)}, f32[1,32,8,256]{3,2,1,0:T(8,128)S(1)}) fusion(f32[2,32,8,256]{3,2,1,0:T(8,128)S(1)} %get-tuple-element.45, f32[1,32,8,256]{3,2,1,0:T(8,128)S(1)} %get-tuple-element.17, f32[2,32,8,256]{3,2,1,0:T(8,128)S(1)} %copy-done, ...), kind=kLoop, calls=%fused_computation.266 | loop fusion | flops 5767168 | bytes 3932160 | tf_op jit(solution)/shard_map/add | solution.py:125
  77.1 0.4 multiply_add_fusion.4
  77.5 0.1 multiply_add_fusion.1
  77.7 0.0 copy-start.1
  77.7 0.1 fusion.143
  77.8 1.9 %collective-permute-start.2 = (f32[2,32,4,256]{3,2,1,0:T(4,128)S(1)}, f32[2,32,4,256]{3,2,1,0:T(4,128)S(1)}, u32[]{:S(2)}, u32[]{:S(2)}) collective-permute-start(f32[2,32,4,256]{3,2,1,0:T(4,128)S(1)} %get-tuple-element.41), channel_id=1, source_target_pairs={{1,0},{2,1},{3,2},{4,3},{5,4},{6,5},{7,6},{8,7},{9,8},{10,9},{11,1... | collective-permute-start | bytes 786440 | tf_op jit(solution)/shard_map/ppermute | solution.py:27
  79.7 5.4 %collective-permute-start.3 = (f32[2,32,4,256]{3,2,1,0:T(4,128)S(1)}, f32[2,32,4,256]{3,2,1,0:T(4,128)S(1)}, u32[]{:S(2)}, u32[]{:S(2)}) collective-permute-start(f32[2,32,4,256]{3,2,1,0:T(4,128)S(1)} %get-tuple-element.42), channel_id=1, source_target_pairs={{0,1},{1,2},{2,3},{3,4},{4,5},{5,6},{6,7},{7,8},{8,9},{9,10},{10,1... | collective-permute-start | bytes 786440 | tf_op jit(solution)/shard_map/ppermute | solution.py:27
  85.1 0.3 select_maximum_fusion
  86.1 0.0 copy-done.1
  86.1 0.7 multiply_select_fusion.partial
  86.8 0.5 collective-permute-done.2
  87.2 1.2 collective-permute-done.3
  88.4 0.3 pad_maximum_fusion
  88.7 1.8 %fusion.43.v_rows = f32[2,32,8,256]{3,2,1,0:T(8,128)} fusion(f32[2,32,8,264]{3,2,1,0:T(8,128)S(1)} %select_maximum_fusion, f32[2,32,12,256]{3,2,1,0:T(8,128)S(1)} %get-tuple-element.40, f32[2,32,12,256]{3,2,1,0:T(8,128)S(1)} %get-tuple-element.39, f32[2,40,8,256]{3,2,1,0:T(8,128)S(1)} %select_maximum_fusion.1, f32[1,32,8,256]{3,2,1,0:T(8,128)S(1)} %get-tuple-element.32, ...), kind=kLoop, calls=%fused_computation.74 | loop fusion | flops 4980736 | bytes 13631488 | tf_op jit(solution)/shard_map/sub | solution.py:450
  90.5 49.7 %backward_exchange.1 = (f32[2,32,8,256]{3,2,1,0:T(8,128)}, f32[256,256]{1,0:T(8,128)}, f32[8,128]{1,0:T(8,128)}) custom-call(f32[32,32,256]{2,1,0:T(8,128)} %get-tuple-element.10.spec, f32[2,32,8,256]{3,2,1,0:T(8,128)} %fusion.43.v_rows, f32[8,128]{1,0:T(8,128)} %multiply_select_fusion.partial, bf16[256,1024]{1,0:T(8,128)(2,1)} %constant.174.clone.t_high, ...), custom_call_target="tpu_custom_call" | custom-call | tf_op jit(solution)/shard_map/backward_exchange/pallas_call | solution.py:421
  140.2 1.3 slice_reduce_fusion
  141.5 2.0 %bitcast_add_fusion = f32[2,1,256,256]{3,2,1,0:T(8,128)} fusion(f32[2,32,8,256]{3,2,1,0:T(8,128)} %get-tuple-element.13, f32[256,256]{1,0:T(8,128)} %get-tuple-element.14), kind=kLoop, calls=%fused_computation.111 | loop fusion | flops 131072 | bytes 1310720 | tf_op jit(solution)/shard_map/add | solution.py:471
  (2 shorter events, 0.0 us)
Async XLA Ops:
  0.6 54.3 %slice-start = ((f32[64,16,512]{2,1,0:T(8,128)}), f32[64,16,1]{2,1,0:T(8,128)S(1)}, s32[]{:S(2)}) async-start(f32[64,16,512]{2,1,0:T(8,128)} %kernel_hat.1), calls=%async_computation | async-start | bytes 1048576 | tf_op jit(solution)/shard_map/slice | solution.py:362
  47.6 15.6 %collective-permute-start = (f32[2,32,4,256]{3,2,1,0:T(4,128)S(1)}, f32[2,32,4,256]{3,2,1,0:T(4,128)S(1)}, u32[]{:S(2)}, u32[]{:S(2)}) collective-permute-start(f32[2,32,4,256]{3,2,1,0:T(4,128)S(1)} %get-tuple-element.46), channel_id=1, source_target_pairs={{1,0},{2,1},{3,2},{4,3},{5,4},{6,5},{7,6},{8,7},{9,8},{10,9},{11,1... | collective-permute-start | bytes 786440 | tf_op jit(solution)/shard_map/ppermute | solution.py:27
  49.5 13.8 %collective-permute-start.1 = (f32[2,32,4,256]{3,2,1,0:T(4,128)S(1)}, f32[2,32,4,256]{3,2,1,0:T(4,128)S(1)}, u32[]{:S(2)}, u32[]{:S(2)}) collective-permute-start(f32[2,32,4,256]{3,2,1,0:T(4,128)S(1)} %get-tuple-element.47), channel_id=1, source_target_pairs={{0,1},{1,2},{2,3},{3,4},{4,5},{5,6},{6,7},{7,8},{8,9},{9,10},{10,1... | collective-permute-start | bytes 786440 | tf_op jit(solution)/shard_map/ppermute | solution.py:27
  56.0 7.1 %copy-start = (f32[2,32,8,256]{3,2,1,0:T(8,128)S(1)}, f32[2,32,8,256]{3,2,1,0:T(8,128)}, u32[]{:S(2)}) copy-start(f32[2,32,8,256]{3,2,1,0:T(8,128)} %get-tuple-element.11) | copy-start | bytes 1572868
  77.7 8.5 %copy-start.1 = (f32[8,128]{1,0:T(8,128)S(1)}, f32[8,128]{1,0:T(8,128)}, u32[]{:S(2)}) copy-start(f32[8,128]{1,0:T(8,128)} %get-tuple-element.12) | copy-start | bytes 12292
  77.8 9.5 %collective-permute-start.2 = (f32[2,32,4,256]{3,2,1,0:T(4,128)S(1)}, f32[2,32,4,256]{3,2,1,0:T(4,128)S(1)}, u32[]{:S(2)}, u32[]{:S(2)}) collective-permute-start(f32[2,32,4,256]{3,2,1,0:T(4,128)S(1)} %get-tuple-element.41), channel_id=1, source_target_pairs={{1,0},{2,1},{3,2},{4,3},{5,4},{6,5},{7,6},{8,7},{9,8},{10,9},{11,1... | collective-permute-start | bytes 786440 | tf_op jit(solution)/shard_map/ppermute | solution.py:27
  79.7 8.7 %collective-permute-start.3 = (f32[2,32,4,256]{3,2,1,0:T(4,128)S(1)}, f32[2,32,4,256]{3,2,1,0:T(4,128)S(1)}, u32[]{:S(2)}, u32[]{:S(2)}) collective-permute-start(f32[2,32,4,256]{3,2,1,0:T(4,128)S(1)} %get-tuple-element.42), channel_id=1, source_target_pairs={{0,1},{1,2},{2,3},{3,4},{4,5},{5,6},{6,7},{7,8},{8,9},{9,10},{10,1... | collective-permute-start | bytes 786440 | tf_op jit(solution)/shard_map/ppermute | solution.py:27
where the time goes:
time: 144 us
  Pallas kernels  102 us (71%)
  other arithmetic  19.5 us (14%)
  starting transfers between devices  14.7 us (10%)
  local copies, waits for them, and re-layouts  3.8 us (3%)
  waiting for transfers between devices  1.64 us (1%)
  between operations  1.46 us (1%)
    pallas_call x1, Pallas kernels, backward_exchange(): pl.pallas_call(functools.partial(backward_kernel, devices), out_shape=(ja...  49.7 us
    pallas_call x1, Pallas kernels, forward_exchange(): pl.pallas_call(functools.partial(forward_kernel, devices), out_shape=(jax...  45.6 us
    ppermute x4, starting transfers between devices, shifted(): lax.ppermute(value, axis, [(source, source + steps) for source in range(l...  14.7 us
    pallas_call x1, Pallas kernels, filtered(): pl.pallas_call(filter_kernel, grid=(1,), out_shape=(jax.ShapeDtypeStruct(...  7.08 us
    add_any x1, other arithmetic, energy_density(): 2.0 * dens_up  4.98 us
    reduce_sum x1, other arithmetic, xc_rows(): return (v_xc, jnp.sum(energy))  3.57 us
  transfers between devices with their start and end apart: 4, of which 2 were waited for; matrix products, arithmetic and copies ran while one was open for 2% of the time, Pallas kernels for 5%

commit v1 on v0

--- a/solution.py
+++ b/solution.py
@@ -392,46 +392,45 @@
 
 
 def backward_kernel(
-    devices, spec, v_rows, partial, t_high, t_low, v_out, h_out, e_out, gathered, sums, sends, receives
+    devices, spec, v_rows, partial, t_high, t_low, out, e_out, v_all, sums, sends, receives
 ):
     me = lax.axis_index("gz")
-    arrived = greet(devices)
-    arrived()
+    greet(devices)()
     finish = remote(
         devices,
         [
-            (lambda peer: spec.at[peer], lambda slot: gathered.at[slot]),
-            (lambda peer: v_rows.at[:, peer], lambda slot: v_out.at[:, slot]),
+            (lambda peer: v_rows.at[:, peer], lambda slot: v_all.at[:, slot]),
             (lambda peer: partial, lambda slot: sums.at[slot]),
         ],
         sends,
         receives,
     )
-    gathered[me] = spec[me]
-    v_out[:, me] = v_rows[:, me]
+    v_all[:, me] = v_rows[:, me]
     sums[me] = partial[...]
+    high, low = split(spec[...].reshape(t_high.shape[1], spec.shape[2]))
+    values = dot(t_high[...], high) + (dot(t_high[...], low) + dot(t_low[...], high))
+    out[0] = values.reshape(out.shape[1:])
     finish()
-    high, low = split(gathered[...].reshape(t_high.shape[1], spec.shape[2]))
-    h_out[...] = dot(t_high[...], high) + (dot(t_high[...], low) + dot(t_low[...], high))
     e_out[...] = jnp.sum(sums[...], axis=0)
+    values = out[0]
+    out[0] = values + v_all[0]
+    out[1] = values + v_all[1]
 
 
 def backward_exchange(devices, spec, v_rows, partial, tables):
-    width_y = tables[0].shape[0]
     return pl.pallas_call(
         functools.partial(backward_kernel, devices),
         out_shape=(
             jax.ShapeDtypeStruct(v_rows.shape, jnp.float32),
-            jax.ShapeDtypeStruct((width_y, spec.shape[2]), jnp.float32),
             jax.ShapeDtypeStruct(partial.shape, jnp.float32),
         ),
         in_specs=[VMEM_SPEC] * 5,
-        out_specs=(VMEM_SPEC,) * 3,
+        out_specs=(VMEM_SPEC,) * 2,
         scratch_shapes=[
-            pltpu.VMEM(spec.shape, jnp.float32),
+            pltpu.VMEM(v_rows.shape, jnp.float32),
             pltpu.VMEM((devices, *partial.shape), jnp.float32),
-            pltpu.SemaphoreType.DMA((3, devices)),
-            pltpu.SemaphoreType.DMA((3, devices)),
+            pltpu.SemaphoreType.DMA((2, devices)),
+            pltpu.SemaphoreType.DMA((2, devices)),
         ],
         compiler_params=pltpu.CompilerParams(
             collective_id=1, has_side_effects=True, vmem_limit_bytes=VMEM_BYTES
@@ -440,11 +439,11 @@
     )(spec, v_rows, partial, *tables)
 
 
-def xc_rows(dens):
+def xc_rows(dens, extended):
     stencil_reach = len(STENCIL)
     grad_z = plane_slope(dens, 1)
     grad_x = plane_slope(dens, 3)
-    grad_y = inner_slope(extend_rows(dens, stencil_reach), 2)
+    grad_y = inner_slope(extended, 2)
     energy, d_dens, flux_z, flux_y, flux_x = xc_fields(dens, grad_z, grad_y, grad_x)
     divergence_y = inner_slope(extend_rows(flux_y, stencil_reach), 2)
     v_xc = d_dens - (plane_slope(flux_z, 1) + divergence_y + plane_slope(flux_x, 3))
@@ -461,15 +460,17 @@
     dens, spec = forward_exchange(
         devices, density.reshape(2, devices, width_y // devices, width_x), forward
     )
-    v_rows, energy_xc = xc_rows(dens)
+    extended = extend_rows(dens, len(STENCIL))
     back, energy_h = filtered(spec, kernel_hat)
+    dens, extended, back = lax.optimization_barrier((dens, extended, back))
+    back = lax.all_to_all(back, "gz", split_axis=0, concat_axis=0, tiled=True)
+    v_rows, energy_xc = xc_rows(dens, extended)
     row = lax.broadcasted_iota(jnp.int32, energy_h.shape, 0)
     partial = jnp.where(
         row == 0, energy_xc / cell_count, energy_h * (0.5 / (8.0 * cell_count) / cell_count)
     )
-    v_xc, hartree, sums = backward_exchange(devices, back, v_rows, partial, inverse)
-    potential = v_xc.reshape(2, 1, width_y, width_x) + hartree[None, None]
-    return (potential, sums[:2, 0])
+    potential, sums = backward_exchange(devices, back, v_rows, partial, inverse)
+    return (potential.reshape(density.shape), sums[:2, 0])
 
 
 def solution(mesh):

time: 144 us -> 126 us (0.88)
  Pallas kernels: 102 us -> 76.4 us
  starting transfers between devices: 14.7 us -> 17.8 us
  local copies, waits for them, and re-layouts: 3.8 us -> 6.53 us
    pallas_call x1, Pallas kernels: 49.7 us -> 23.7 us  [backward_exchange(): pl.pallas_call(functools.partial(backward_kernel, devices), out_shape=(ja...]
    all_to_all x0 -> x1, starting transfers between devices: none -> 5.85 us  [per_device(): back = lax.all_to_all(back, 'gz', split_axis=0, concat_axis=0, tiled=True)]
    ppermute x4, starting transfers between devices: 14.7 us -> 11.9 us  [shifted(): lax.ppermute(value, axis, [(source, source + steps) for source in range(l...]
    unnamed x6 -> x8, local copies, waits for them, and re-layouts: 0.49 us -> 3.29 us
    add x1 -> x0, other arithmetic: 1.95 us -> none  [per_device(): potential = v_xc.reshape(2, 1, width_y, width_x) + hartree[None, None]]
  transfers between devices with their start and end apart: 4 -> 5, of which waited for: 2 -> 1; matrix products, arithmetic and copies ran while one was open for 2% -> 17% of each run, Pallas kernels for 5% -> 6%
where the time goes in v1:
time: 126 us
  Pallas kernels  76.4 us (61%)
  other arithmetic  20.8 us (17%)
  starting transfers between devices  17.8 us (14%)
  local copies, waits for them, and re-layouts  6.53 us (5%)
  waiting for transfers between devices  2.95 us (2%)
  between operations  1.45 us (1%)
    pallas_call x1, Pallas kernels, forward_exchange(): pl.pallas_call(functools.partial(forward_kernel, devices), out_shape=(jax...  45.6 us
    pallas_call x1, Pallas kernels, backward_exchange(): pl.pallas_call(functools.partial(backward_kernel, devices), out_shape=(ja...  23.7 us
    ppermute x4, starting transfers between devices, shifted(): lax.ppermute(value, axis, [(source, source + steps) for source in range(l...  11.9 us
    pallas_call x1, Pallas kernels, filtered(): pl.pallas_call(filter_kernel, grid=(1,), out_shape=(jax.ShapeDtypeStruct(...  7.07 us
    all_to_all x1, starting transfers between devices, per_device(): back = lax.all_to_all(back, 'gz', split_axis=0, concat_axis=0, tiled=True)  5.85 us
    add_any x1, other arithmetic, energy_density(): 2.0 * dens_up  4.8 us
    reduce_sum x1, other arithmetic, xc_rows(): return (v_xc, jnp.sum(energy))  3.57 us
    unnamed x8, local copies, waits for them, and re-layouts  3.29 us
  transfers between devices with their start and end apart: 5, of which 1 were waited for; matrix products, arithmetic and copies ran while one was open for 17% of the time, Pallas kernels for 6%

profile of v1, /device:TPU:15, one launch (start us, length us, event | category | flops | bytes accessed | tf_op | source)
XLA Modules:
  0.0 125.9 jit_solution(14930317392406960039)
XLA Ops:
  0.6 0.0 slice-start
  0.6 45.6 %forward_exchange.1 = (f32[2,32,8,256]{3,2,1,0:T(8,128)}, f32[32,32,256]{2,1,0:T(8,128)}) custom-call(f32[2,32,8,256]{3,2,1,0:T(8,128)} %bitcast.101, bf16[1024,256]{1,0:T(8,128)(2,1)} %constant.168.clone.t_high, bf16[1024,256]{1,0:T(8,128)(2,1)} %constant.169.clone.t_low), custom_call_target="tpu_custom_call" | custom-call | tf_op jit(solution)/shard_map/forward_exchange/pallas_call | solution.py:291
  46.3 1.3 %fusion.185 = (f32[2,32,4,256]{3,2,1,0:T(4,128)S(1)}, f32[2,32,4,256]{3,2,1,0:T(4,128)S(1)}) fusion(f32[2,32,8,256]{3,2,1,0:T(8,128)} %get-tuple-element.15), kind=kLoop, calls=%fused_computation.329 | loop fusion | bytes 1048576 | tf_op jit(solution)/shard_map/slice | solution.py:159
  47.6 1.9 %collective-permute-start = (f32[2,32,4,256]{3,2,1,0:T(4,128)S(1)}, f32[2,32,4,256]{3,2,1,0:T(4,128)S(1)}, u32[]{:S(2)}, u32[]{:S(2)}) collective-permute-start(f32[2,32,4,256]{3,2,1,0:T(4,128)S(1)} %get-tuple-element.53), channel_id=1, source_target_pairs={{0,1},{1,2},{2,3},{3,4},{4,5},{5,6},{6,7},{7,8},{8,9},{9,10},{10,1... | collective-permute-start | bytes 786440 | tf_op jit(solution)/shard_map/ppermute | solution.py:27
  49.5 2.4 %collective-permute-start.1 = (f32[2,32,4,256]{3,2,1,0:T(4,128)S(1)}, f32[2,32,4,256]{3,2,1,0:T(4,128)S(1)}, u32[]{:S(2)}, u32[]{:S(2)}) collective-permute-start(f32[2,32,4,256]{3,2,1,0:T(4,128)S(1)} %get-tuple-element.54), channel_id=1, source_target_pairs={{1,0},{2,1},{3,2},{4,3},{5,4},{6,5},{7,6},{8,7},{9,8},{10,9},{11,1... | collective-permute-start | bytes 786440 | tf_op jit(solution)/shard_map/ppermute | solution.py:27
  51.9 0.0 slice-done
  51.9 0.4 copy.16
  52.4 0.6 pad.18.edge
  53.0 0.0 copy-start
  53.0 7.1 %kernel_filter.1 = (f32[32,32,256]{2,1,0:T(8,128)}, f32[8,128]{1,0:T(8,128)}) custom-call(f32[32,32,256]{2,1,0:T(8,128)} %get-tuple-element.12.spec, f32[64,16,512]{2,1,0:T(8,128)} %kernel_hat.1, f32[64,128]{1,0:T(8,128)} %pad.18.edge, bf16[256,512]{1,0:T(8,128)(2,1)} %constant.170.clone.tx_high, bf16[256,512]{1,0:T(8,128)(2,1)} %constant.171.clone.tx_low, ...), custom_call_target="tpu_custom_call" | custom-call | flops 10000000000 | bytes 4000000 | tf_op jit(solution)/shard_map/kernel_filter/pallas_call | solution.py:365
  60.1 0.0 collective-permute-done
  60.1 0.0 collective-permute-done.1
  60.1 0.0 copy-done
  60.1 0.2 pad_maximum_fusion
  60.3 5.9 %all-to-all-start = ((f32[32,32,256]{2,1,0:T(8,128)}), f32[32,32,256]{2,1,0:T(8,128)S(1)}, u32[]{:S(2)}, u32[]{:S(2)}) async-start(f32[32,32,256]{2,1,0:T(8,128)} %get-tuple-element.14), calls=%async_computation | async-start | bytes 2097152 | tf_op jit(solution)/shard_map/all_to_all | solution.py:466
  66.2 1.7 %fusion.19 = (f32[2,32,8,256]{3,2,1,0:T(8,128)S(1)}, f32[2,32,8,256]{3,2,1,0:T(8,128)S(1)}, f32[2,32,8,256]{3,2,1,0:T(8,128)S(1)}) fusion(f32[2,32,8,256]{3,2,1,0:T(8,128)S(1)} %copy-done, f32[2,32,16,256]{3,2,1,0:T(8,128)S(1)} %pad_maximum_fusion), kind=kLoop, calls=%fused_computation.44 | loop fusion | flops 4718592 | bytes 6291456 | tf_op jit(solution)/shard_map/div | solution.py:48
  67.9 3.6 %fusion.134 = (f32[]{:T(128)}, f32[1,32,8,256]{3,2,1,0:T(8,128)S(1)}, f32[1,32,8,256]{3,2,1,0:T(8,128)S(1)}, f32[1,32,8,256]{3,2,1,0:T(8,128)S(1)}, f32[1,32,8,256]{3,2,1,0:T(8,128)S(1)}) fusion(f32[2,32,8,256]{3,2,1,0:T(8,128)S(1)} %copy-done, f32[2,32,8,256]{3,2,1,0:T(8,128)S(1)} %get-tuple-element.51, f32[2,32,8,256]{3,2,1,0:T(8,128)S(1)} %get-tuple-element.55, ...), kind=kLoop, calls=%fused_computation.208 | loop fusion | flops 9633791 | bytes 3145732 | tf_op jit(solution)/shard_map/reduce_sum | solution.py:450
  71.4 1.6 %negate_divide_fusion = (f32[1,32,8,256]{3,2,1,0:T(8,128)S(1)}, f32[1,32,8,256]{3,2,1,0:T(8,128)S(1)}) fusion(f32[1,32,8,256]{3,2,1,0:T(8,128)S(1)} %get-tuple-element.28, f32[2,32,8,256]{3,2,1,0:T(8,128)S(1)} %copy-done), kind=kLoop, calls=%fused_computation.310 | loop fusion | flops 4980736 | bytes 1310720 | tf_op jit(solution)/shard_map/jvp()/div | solution.py:107
  73.0 4.8 %multiply_add_fusion.8 = (f32[1,32,8,256]{3,2,1,0:T(8,128)S(1)}, f32[1,32,8,256]{3,2,1,0:T(8,128)S(1)}, f32[1,32,8,256]{3,2,1,0:T(8,128)S(1)}, f32[1,32,8,256]{3,2,1,0:T(8,128)S(1)}) fusion(f32[1,32,8,256]{3,2,1,0:T(8,128)S(1)} %get-tuple-element.25, f32[2,32,8,256]{3,2,1,0:T(8,128)S(1)} %copy-done, f32[1,32,8,256]{3,2,1,0:T(8,128)S(1)} %get-tuple-element.28, ...), kind=kLoop, calls=%fused_computation.252 | loop fusion | flops 22478848 | bytes 2883584 | tf_op jit(solution)/shard_map/transpose(jvp())/add_any | solution.py:80
  77.8 2.5 %multiply_add_fusion.5 = (f32[1,32,8,256]{3,2,1,0:T(8,128)S(1)}, f32[1,32,8,256]{3,2,1,0:T(8,128)S(1)}, f32[1,32,8,256]{3,2,1,0:T(8,128)S(1)}, f32[1,32,8,256]{3,2,1,0:T(8,128)}) fusion(f32[2,32,8,256]{3,2,1,0:T(8,128)S(1)} %get-tuple-element.52, f32[1,32,8,256]{3,2,1,0:T(8,128)S(1)} %get-tuple-element.25, f32[2,32,8,256]{3,2,1,0:T(8,128)S(1)} %copy-done, ...), kind=kLoop, calls=%fused_computation.245 | loop fusion | flops 5767168 | bytes 3932160 | tf_op jit(solution)/shard_map/add | solution.py:125
  80.3 0.4 multiply_add_fusion.4
  80.7 0.1 multiply_add_fusion.1
  80.8 0.0 copy-start.2
  80.8 0.9 fusion.128
  81.7 2.3 %collective-permute-start.2 = (f32[2,32,4,256]{3,2,1,0:T(4,128)}, f32[2,32,4,256]{3,2,1,0:T(4,128)}, u32[]{:S(2)}, u32[]{:S(2)}) collective-permute-start(f32[2,32,4,256]{3,2,1,0:T(4,128)} %get-tuple-element.49), channel_id=1, source_target_pairs={{1,0},{2,1},{3,2},{4,3},{5,4},{6,5},{7,6},{8,7},{9,8},{10,9},{11,1... | collective-permute-start | bytes 786440 | tf_op jit(solution)/shard_map/ppermute | solution.py:27
  84.0 5.3 %collective-permute-start.3 = (f32[2,32,4,256]{3,2,1,0:T(4,128)}, f32[2,32,4,256]{3,2,1,0:T(4,128)}, u32[]{:S(2)}, u32[]{:S(2)}) collective-permute-start(f32[2,32,4,256]{3,2,1,0:T(4,128)} %get-tuple-element.50), channel_id=1, source_target_pairs={{0,1},{1,2},{2,3},{3,4},{4,5},{5,6},{6,7},{7,8},{8,9},{9,10},{10,1... | collective-permute-start | bytes 786440 | tf_op jit(solution)/shard_map/ppermute | solution.py:27
  89.3 0.3 select_maximum_fusion
  90.3 0.0 copy-done.2
  90.3 0.6 multiply_select_fusion.partial
  90.9 2.9 %collective-permute-done.2 = f32[2,32,4,256]{3,2,1,0:T(4,128)} collective-permute-done((f32[2,32,4,256]{3,2,1,0:T(4,128)}, f32[2,32,4,256]{3,2,1,0:T(4,128)}, u32[]{:S(2)}, u32[]{:S(2)}) %collective-permute-start.2) | collective-permute-done | bytes 262176 | tf_op jit(solution)/shard_map/ppermute | solution.py:27
  93.9 0.0 collective-permute-done.3
  93.9 1.3 %pad_maximum_fusion.1 = (f32[2,32,12,256]{3,2,1,0:T(8,128)S(1)}, f32[2,32,12,256]{3,2,1,0:T(8,128)S(1)}) fusion(f32[2,32,4,256]{3,2,1,0:T(4,128)} %collective-permute-done.2, f32[1,32,8,256]{3,2,1,0:T(8,128)S(1)} %get-tuple-element.45, f32[1,32,8,256]{3,2,1,0:T(8,128)S(1)} %get-tuple-element.46, f32[2,32,4,256]{3,2,1,0:T(4,128)} %collective-permute-done.3), kind=kLoop, calls=%fused_computation.11 | loop fusion | flops 786432 | bytes 2621440 | tf_op jit(solution)/shard_map/concatenate | solution.py:161
  95.2 2.8 %fusion.30.v_rows = f32[2,32,8,256]{3,2,1,0:T(8,128)} fusion(f32[2,32,8,264]{3,2,1,0:T(8,128)S(1)} %select_maximum_fusion, f32[2,32,12,256]{3,2,1,0:T(8,128)S(1)} %get-tuple-element.48, f32[2,32,12,256]{3,2,1,0:T(8,128)S(1)} %get-tuple-element.47, f32[2,40,8,256]{3,2,1,0:T(8,128)S(1)} %select_maximum_fusion.1, f32[1,32,8,256]{3,2,1,0:T(8,128)} %get-tuple-element.40, ...), kind=kLoop, calls=%fused_computation.56 | loop fusion | flops 4980736 | bytes 13631488 | tf_op jit(solution)/shard_map/sub | solution.py:449
  98.0 0.0 all-to-all-done.spec
  98.0 0.0 copy-start.1
  98.0 1.0 copy-done.1
  99.0 23.7 %backward_exchange.1 = (f32[2,32,8,256]{3,2,1,0:T(8,128)}, f32[8,128]{1,0:T(8,128)}) custom-call(f32[32,32,256]{2,1,0:T(8,128)} %copy-done.1, f32[2,32,8,256]{3,2,1,0:T(8,128)} %fusion.30.v_rows, f32[8,128]{1,0:T(8,128)} %multiply_select_fusion.partial, bf16[256,1024]{1,0:T(8,128)(2,1)} %constant.174.clone.t_high, bf16[256,1024]{1,0:T(8,128)(2,1)} %constant.175.clone.t_low), custom_call_target="tpu_custom_call" | custom-call | tf_op jit(solution)/shard_map/backward_exchange/pallas_call | solution.py:421
  122.7 1.3 %slice_reduce_fusion = f32[2]{0:T(128)} fusion(f32[8,128]{1,0:T(8,128)} %get-tuple-element.19), kind=kLoop, calls=%fused_computation.325 | loop fusion | bytes 16 | tf_op jit(solution)/shard_map/slice | solution.py:473
  124.0 1.9 %copy.18 = f32[2,1,256,256]{3,2,1,0:T(8,128)} copy(f32[2,1,256,256]{3,2,1,0:T(8,128)} %bitcast.102) | data formatting | bytes 1048576
  (2 shorter events, 0.0 us)
Async XLA Ops:
  0.6 51.3 %slice-start = ((f32[64,16,512]{2,1,0:T(8,128)}), f32[64,16,1]{2,1,0:T(8,128)S(1)}, s32[]{:S(2)}) async-start(f32[64,16,512]{2,1,0:T(8,128)} %kernel_hat.1), calls=%async_computation.1 | async-start | bytes 1048576 | tf_op jit(solution)/shard_map/slice | solution.py:362
  47.6 12.5 %collective-permute-start = (f32[2,32,4,256]{3,2,1,0:T(4,128)S(1)}, f32[2,32,4,256]{3,2,1,0:T(4,128)S(1)}, u32[]{:S(2)}, u32[]{:S(2)}) collective-permute-start(f32[2,32,4,256]{3,2,1,0:T(4,128)S(1)} %get-tuple-element.53), channel_id=1, source_target_pairs={{0,1},{1,2},{2,3},{3,4},{4,5},{5,6},{6,7},{7,8},{8,9},{9,10},{10,1... | collective-permute-start | bytes 786440 | tf_op jit(solution)/shard_map/ppermute | solution.py:27
  49.5 10.6 %collective-permute-start.1 = (f32[2,32,4,256]{3,2,1,0:T(4,128)S(1)}, f32[2,32,4,256]{3,2,1,0:T(4,128)S(1)}, u32[]{:S(2)}, u32[]{:S(2)}) collective-permute-start(f32[2,32,4,256]{3,2,1,0:T(4,128)S(1)} %get-tuple-element.54), channel_id=1, source_target_pairs={{1,0},{2,1},{3,2},{4,3},{5,4},{6,5},{7,6},{8,7},{9,8},{10,9},{11,1... | collective-permute-start | bytes 786440 | tf_op jit(solution)/shard_map/ppermute | solution.py:27
  53.0 7.1 %copy-start = (f32[2,32,8,256]{3,2,1,0:T(8,128)S(1)}, f32[2,32,8,256]{3,2,1,0:T(8,128)}, u32[]{:S(2)}) copy-start(f32[2,32,8,256]{3,2,1,0:T(8,128)} %get-tuple-element.15) | copy-start | bytes 1572868
  60.3 37.7 %all-to-all-start = ((f32[32,32,256]{2,1,0:T(8,128)}), f32[32,32,256]{2,1,0:T(8,128)S(1)}, u32[]{:S(2)}, u32[]{:S(2)}) async-start(f32[32,32,256]{2,1,0:T(8,128)} %get-tuple-element.14), calls=%async_computation | async-start | bytes 2097152 | tf_op jit(solution)/shard_map/all_to_all | solution.py:466
  80.8 9.4 %copy-start.2 = (f32[8,128]{1,0:T(8,128)S(1)}, f32[8,128]{1,0:T(8,128)}, u32[]{:S(2)}) copy-start(f32[8,128]{1,0:T(8,128)} %get-tuple-element.17) | copy-start | bytes 12292
  81.7 12.2 %collective-permute-start.2 = (f32[2,32,4,256]{3,2,1,0:T(4,128)}, f32[2,32,4,256]{3,2,1,0:T(4,128)}, u32[]{:S(2)}, u32[]{:S(2)}) collective-permute-start(f32[2,32,4,256]{3,2,1,0:T(4,128)} %get-tuple-element.49), channel_id=1, source_target_pairs={{1,0},{2,1},{3,2},{4,3},{5,4},{6,5},{7,6},{8,7},{9,8},{10,9},{11,1... | collective-permute-start | bytes 786440 | tf_op jit(solution)/shard_map/ppermute | solution.py:27
  84.0 9.9 %collective-permute-start.3 = (f32[2,32,4,256]{3,2,1,0:T(4,128)}, f32[2,32,4,256]{3,2,1,0:T(4,128)}, u32[]{:S(2)}, u32[]{:S(2)}) collective-permute-start(f32[2,32,4,256]{3,2,1,0:T(4,128)} %get-tuple-element.50), channel_id=1, source_target_pairs={{0,1},{1,2},{2,3},{3,4},{4,5},{5,6},{6,7},{7,8},{8,9},{9,10},{10,1... | collective-permute-start | bytes 786440 | tf_op jit(solution)/shard_map/ppermute | solution.py:27
  98.0 1.0 copy-start.1
